TPU v7x, 32 devices: a 4x4x1 block of a 4x4x8 slice. The times are simulated.
32 devices in a mesh: batch: 1 (over z), dap: 32 (over y, x, core).
Axes of the slice: x: 4, y: 4, z: 1, core: 2. Of those that a mesh axis runs over, the one named last changes fastest.
The devices are a block of a 4x4x8 slice.
Arguments:
- z_pair: bfloat16 [512, 512, 128], P(('batch', 'dap'))
- msa_feat: bfloat16 [512, 512, 64], P(None, ('batch', 'dap'))
- ln_scale: bfloat16 [64], replicated
- ln_offset: bfloat16 [64], replicated
- w_a: bfloat16 [64, 32], replicated
- b_a: bfloat16 [32], replicated
- w_b: bfloat16 [64, 32], replicated
- b_b: bfloat16 [32], replicated
- w_out: bfloat16 [1024, 128], replicated
- b_out: bfloat16 [128], replicated
Outputs:
- output: bfloat16 [512, 512, 128], P(('batch', 'dap'))
All inputs are finite; a program needn't handle non-finite values.
Results may differ from a plain program's by a relative error of at most 0.001.
Values are sent between devices in bfloat16 or wider.
A program may use at most 768 MiB of HBM per device.

v0:
```python
import jax
import jax.numpy as jnp
from jax import lax
from jax.sharding import PartitionSpec as P

LN_EPS = 1e-5
ROW_BUDGET = 8192


def layer_norm(array_b8, ln_scale, ln_offset):
    value_a7 = array_b8.astype(jnp.float32)
    mean_val = jnp.mean(value_a7, axis=-1, keepdims=True)
    centred = value_a7 - mean_val
    var_val = jnp.mean(centred * centred, axis=-1, keepdims=True)
    normed = centred * lax.rsqrt(var_val + LN_EPS)
    return (normed * ln_scale.astype(jnp.float32) + ln_offset.astype(jnp.float32)).astype(jnp.bfloat16)


def project(local_c8, weight, bias_vec):
    out_f32 = jnp.einsum('snm,mc->snc', local_c8, weight, preferred_element_type=jnp.float32)
    return (out_f32 + bias_vec.astype(jnp.float32)).astype(jnp.bfloat16)


def outer_update(z_rows, proj_a, full_b, w_out, b_out):
    n_seq, n_loc, hid_dim = proj_a.shape
    n_res = full_b.shape[1]
    pair_dim = z_rows.shape[2]
    row_tile = min(n_loc, max(1, ROW_BUDGET // n_res))
    w_cube = w_out.reshape(hid_dim, hid_dim, pair_dim)
    bias_out = b_out.astype(jnp.float32)
    inv_seq = 1.0 / n_seq

    def tile_body(tile_idx, z_acc):
        row_start = tile_idx * row_tile
        a_tile = lax.dynamic_slice_in_dim(proj_a, row_start, row_tile, axis=1)
        z_tile = lax.dynamic_slice_in_dim(z_acc, row_start, row_tile, axis=0)
        outer_prod = jnp.einsum('sic,sjd->icjd', a_tile, full_b, preferred_element_type=jnp.float32)
        outer_prod = (outer_prod * inv_seq).astype(jnp.bfloat16)
        update = jnp.einsum('icjd,cdz->ijz', outer_prod, w_cube, preferred_element_type=jnp.float32) + bias_out
        new_tile = (z_tile.astype(jnp.float32) + update).astype(jnp.bfloat16)
        return lax.dynamic_update_slice_in_dim(z_acc, new_tile, row_start, axis=0)

    return lax.fori_loop(0, n_loc // row_tile, tile_body, z_rows)


def solution(mesh):
    row_spec = P(('batch', 'dap'))
    col_spec = P(None, ('batch', 'dap'))
    rep_spec = P()

    def local_update(z_rows, value_a8, ln_scale, ln_offset, w_a, b_a, w_b, b_b, w_out, b_out):
        local_c8 = layer_norm(value_a8, ln_scale, ln_offset)
        proj_a = project(local_c8, w_a, b_a)
        proj_b = project(local_c8, w_b, b_b)
        full_b = lax.all_gather(proj_b, 'dap', axis=1, tiled=True)
        return outer_update(z_rows, proj_a, full_b, w_out, b_out)

    return jax.shard_map(local_update, mesh=mesh, in_specs=(row_spec, col_spec) + (rep_spec,) * 8, out_specs=row_spec, check_vma=False)
```

profile of v0, /device:TPU:97, one launch (start us, length us, event | category | flops | bytes accessed | tf_op | source)
XLA Modules:
  0.0 131.2 jit_solution(595953639632253539)
XLA Ops:
  6.5 0.0 copy-start
  6.6 0.0 copy-start.1
  6.6 0.0 copy-start.5
  6.6 0.0 copy-start.6
  6.6 0.0 copy-start.7
  6.6 0.0 copy-start.3
  6.6 0.1 all-gather.2.cloned.1.call-start
  6.6 1.5 %convert_reduce_fusion = f32[512,16]{0,1:T(8,128)S(1)} fusion(bf16[512,16,64]{0,2,1:T(8,128)(2,1)} %param.11), kind=kLoop, calls=%fused_computation.10 | loop fusion | flops 1040384 | bytes 1081344 | tf_op jit(solution)/shard_map/reduce_sum | solution.py:12
  8.2 0.0 copy-start.8
  8.2 0.0 copy-start.9
  8.2 0.0 copy-start.4
  8.2 1.6 %fusion.9 = f32[512,16]{0,1:T(8,128)S(1)} fusion(bf16[512,16,64]{0,2,1:T(8,128)(2,1)} %param.11, f32[512,16]{0,1:T(8,128)S(1)} %broadcast_multiply_fusion), kind=kLoop, calls=%fused_computation.13 | loop fusion | flops 2088960 | bytes 1114112 | tf_op jit(solution)/shard_map/reduce_sum | solution.py:14
  9.8 0.0 copy-done.5
  9.8 0.0 copy-done.6
  9.8 0.0 copy-done.7
  9.9 0.0 copy-done.1
  9.9 0.0 copy-done.3
  9.9 1.4 %fusion.14 = bf16[512,16,32]{0,2,1:T(8,128)(2,1)} fusion(f32[32]{0:T(128)S(1)} %convert_element_type.46, bf16[64,32]{0,1:T(8,128)(2,1)S(1)} %copy-done.3, bf16[512,16,64]{0,2,1:T(8,128)(2,1)S(1)} %copy-done.1, f32[64]{0:T(128)S(1)} %convert_element_type.42, f32[64]{0:T(128)S(1)} %convert_element_type.41, f32[512,16]{0,1:T(8,128)S(1)} %add_rsqrt_fusion, ...), kind=kOutput, calls=%fused_computation.20 | convolution fusion | flops 37224448 | bytes 1643136 | tf_op jit(solution)/shard_map/snm,mc->snc/dot_general | solution.py:20
  11.3 0.1 all-gather.2.cloned.1.call-update
  11.3 0.0 copy-done.8
  11.4 0.0 copy-done.9
  11.4 0.0 copy-start.2
  11.4 71.6 %all-gather.2.cloned.1.call-done = bf16[512,512,32]{0,2,1:T(8,128)(2,1)} async-done(((bf16[512,16,32]{0,2,1:T(8,128)(2,1)}), bf16[512,512,32]{0,2,1:T(8,128)(2,1)}) %all-gather.2.cloned.1.call-update) | async-done | bytes 16777232 | tf_op jit(solution)/shard_map/all_gather | solution.py:55
  83.0 0.0 copy-done.4
  83.0 24.6 %fusion.1 = f32[16,32,512,32]{2,1,3,0:T(8,128)} fusion(bf16[512,512,32]{0,2,1:T(8,128)(2,1)} %all-gather.2.cloned.1.call-done, f32[32]{0:T(128)S(1)} %convert_element_type.44, bf16[64,32]{0,1:T(8,128)(2,1)S(1)} %copy-done.4, bf16[512,16,64]{0,2,1:T(8,128)(2,1)S(1)} %copy-done.1, f32[64]{0:T(128)S(1)} %convert_element_type.42, ...), kind=kOutput, calls=%fused_computation.2 | convolution fusion | flops 8627159040 | bytes 51450496 | tf_op jit(solution)/shard_map/while/body/eval_jaxpr/sic,sjd->icjd/dot_general | solution.py:37
  107.6 0.0 copy-done
  107.6 0.0 copy-done.2
  107.6 16.7 %fusion.6 = bf16[16,512,128]{2,1,0:T(8,128)(2,1)} fusion(bf16[16,512,128]{2,1,0:T(8,128)(2,1)S(1)} %copy-done.2, f32[16,32,512,32]{2,1,3,0:T(8,128)} %fusion.1, f32[128]{0:T(128)S(1)} %convert_element_type.49, bf16[32,32,128,1]{2,1,0,3:T(8,128)(2,1)S(1)} %bitcast.26), kind=kOutput, calls=%fused_computation.8 | convolution fusion | flops 2168455168 | bytes 38011392 | tf_op jit(solution)/shard_map/while/body/eval_jaxpr/icjd,cdz->ijz/dot_general | solution.py:39
  (7 shorter events, 0.0 us)
Async XLA Ops:
  6.5 101.0 %copy-start = (bf16[1024,128]{1,0:T(8,128)(2,1)S(1)}, bf16[1024,128]{1,0:T(8,128)(2,1)}, u32[]{:S(2)}) copy-start(bf16[1024,128]{1,0:T(8,128)(2,1)} %param.18) | copy-start | bytes 786436
  6.6 3.3 %copy-start.1 = (bf16[512,16,64]{0,2,1:T(8,128)(2,1)S(1)}, bf16[512,16,64]{0,2,1:T(8,128)(2,1)}, u32[]{:S(2)}) copy-start(bf16[512,16,64]{0,2,1:T(8,128)(2,1)} %param.11) | copy-start | bytes 3145732
  6.6 3.2 %copy-start.5 = (bf16[64]{0:T(256)(128)(2,1)S(1)}, bf16[64]{0:T(256)(128)(2,1)}, u32[]{:S(2)}) copy-start(bf16[64]{0:T(256)(128)(2,1)} %param.12) | copy-start | bytes 388
  6.6 3.3 %copy-start.6 = (bf16[64]{0:T(256)(128)(2,1)S(1)}, bf16[64]{0:T(256)(128)(2,1)}, u32[]{:S(2)}) copy-start(bf16[64]{0:T(256)(128)(2,1)} %param.13) | copy-start | bytes 388
  6.6 3.3 %copy-start.7 = (bf16[32]{0:T(256)(128)(2,1)S(1)}, bf16[32]{0:T(256)(128)(2,1)}, u32[]{:S(2)}) copy-start(bf16[32]{0:T(256)(128)(2,1)} %param.17) | copy-start | bytes 196
  6.6 3.3 %copy-start.3 = (bf16[64,32]{0,1:T(8,128)(2,1)S(1)}, bf16[64,32]{0,1:T(8,128)(2,1)}, u32[]{:S(2)}) copy-start(bf16[64,32]{0,1:T(8,128)(2,1)} %param.16) | copy-start | bytes 12292
  6.6 76.4 %all-gather.2.cloned.1.call-start = ((), (), s32[]{:S(2)}) async-start(), calls=%async_computation | async-start | bytes 17301504 | tf_op jit(solution)/shard_map/all_gather | solution.py:55
  8.2 3.2 %copy-start.8 = (bf16[32]{0:T(256)(128)(2,1)S(1)}, bf16[32]{0:T(256)(128)(2,1)}, u32[]{:S(2)}) copy-start(bf16[32]{0:T(256)(128)(2,1)} %param.15) | copy-start | bytes 196
  8.2 3.2 %copy-start.9 = (bf16[128]{0:T(256)(128)(2,1)S(1)}, bf16[128]{0:T(256)(128)(2,1)}, u32[]{:S(2)}) copy-start(bf16[128]{0:T(256)(128)(2,1)} %param.19) | copy-start | bytes 772
  8.2 74.8 %copy-start.4 = (bf16[64,32]{0,1:T(8,128)(2,1)S(1)}, bf16[64,32]{0,1:T(8,128)(2,1)}, u32[]{:S(2)}) copy-start(bf16[64,32]{0,1:T(8,128)(2,1)} %param.14) | copy-start | bytes 12292
  11.4 96.2 %copy-start.2 = (bf16[16,512,128]{2,1,0:T(8,128)(2,1)S(1)}, bf16[16,512,128]{2,1,0:T(8,128)(2,1)}, u32[]{:S(2)}) copy-start(bf16[16,512,128]{2,1,0:T(8,128)(2,1)} %param.10) | copy-start | bytes 6291460
Sparse Core Ops, SparseCore 0:
  11.5 71.5 all-gather.1
where the time goes:
time: 131 us
  waiting for transfers between devices  71.7 us (55%)
  matrix products  42.7 us (33%)
  between operations  13.6 us (10%)
  other arithmetic  3.12 us (2%)
    all_gather x1, waiting for transfers between devices, local_update(): full_b = lax.all_gather(proj_b, 'dap', axis=1, tiled=True)  71.6 us
    dot_general x1, matrix products, tile_body(): jnp.einsum('sic,sjd->icjd', a_tile, full_b, preferred_element_type=jnp.fl...  24.6 us
    dot_general x1, matrix products, tile_body(): jnp.einsum('icjd,cdz->ijz', outer_prod, w_cube, preferred_element_type=jn...  16.7 us
  transfers between devices with their start and end apart: 1, of which 1 were waited for; matrix products, arithmetic and copies ran while one was open for 0% of the time, Pallas kernels for 0%

commit v1 on v0

v1 whole, which is shorter than its diff:
```python
import functools
import math

import jax
import jax.numpy as jnp
from jax import lax
from jax.experimental import pallas as pl
from jax.experimental.pallas import tpu as pltpu
from jax.sharding import PartitionSpec as P

LN_EPS = 1e-5
CORES = 2
PARTS = 4
PARTNER_LAG = 3
MESH = pl.DeviceIdType.MESH
F32 = jnp.float32
BF16 = jnp.bfloat16


def forwards(block, part, side):
    first, second = block
    low = part < PARTS // 2
    hops = []
    if second == 0:
        if first == 0 or (first == side - 1 and low):
            hops.append(("A+", ((first - 1) % side, second)))
        if first == 0 or (first == 1 and not low):
            hops.append(("A-", ((first + 1) % side, second)))
        hops.append(("B+", (first, side - 1)))
        hops.append(("B-", (first, 1)))
    elif second == side - 1 and low:
        hops.append(("B+", (first, (second - 1) % side)))
    elif second == 1 and not low:
        hops.append(("B-", (first, (second + 1) % side)))
    return hops


def arrival_order(side):
    queues = {d: [] for d in ("A+", "A-", "B+", "B-")}
    for part in range(PARTS):
        for d, name in forwards((0, 0), part, side):
            queues[d].append((name, part))
    order, turn = [], {"+": 0, "-": 0}
    pending = []
    while any(queues.values()) or pending:
        for name, part in pending:
            order.append((name, part))
            for d, there in forwards(name, part, side):
                queues[d].append((there, part))
        pending = []
        for sign in "+-":
            pick = "AB"[turn[sign]] + sign
            if not queues[pick]:
                pick = "BA"[turn[sign]] + sign
            if queues[pick]:
                pending.append(queues[pick].pop(0))
            turn[sign] = 1 - turn[sign]
    return order


def plan(side):
    own, other = "own", "other"
    units = [(own, (0, 0)), (other, (0, 0))]
    before = [[], []]
    backlog, count, waiting = [], {}, []
    for index, (name, part) in enumerate(arrival_order(side)):
        waiting.append((name, part))
        count[name] = count.get(name, 0) + 1
        if count[name] == PARTS:
            backlog.append((index, own, name))
            backlog.append((index + PARTNER_LAG, other, name))
            backlog.sort(key=lambda item: item[0])
        if backlog and backlog[0][0] <= index:
            _, kind, done = backlog.pop(0)
            units.append((kind, done))
            before.append(waiting)
            waiting = []
    for _, kind, done in backlog:
        units.append((kind, done))
        before.append(waiting)
        waiting = []
    return units, before


def column(row, size):
    shape = (size, size)
    eye = lax.broadcasted_iota(jnp.int32, shape, 0) == lax.broadcasted_iota(jnp.int32, shape, 1)
    return jnp.sum(jnp.where(eye, jnp.broadcast_to(row, shape), 0.0), axis=1, keepdims=True)


def dispatch(index, low, high, actions):
    if not any(actions[low:high]):
        return
    if high - low == 1:
        for action in actions[low]:
            action()
        return
    mid = (low + high) // 2
    if any(actions[low:mid]):
        pl.when(index < mid)(lambda: dispatch(index, low, mid, actions))
    if any(actions[mid:high]):
        pl.when(index >= mid)(lambda: dispatch(index, mid, high, actions))


def kernel(side, units, before, z_hbm, m_hbm, scale_hbm, offset_hbm, wa_hbm, ba_hbm, wb_hbm, bb_hbm, wo_hbm, bo_hbm, out_ref,
           m_ref, scale_ref, offset_ref, wa_ref, ba_ref, wb_ref, bb_ref, wo_ref, bo_ref, z_ref,
           held, a_rows, a_cols, outer, lhs, upd, in_sem, m_sem, wo_sem, z_sem, send_sem, part_sem, block_sem):
    n_loc, msa_dim, n_seq = m_ref.shape
    hid = wa_ref.shape[0]
    rows = n_loc * hid
    part_rows = rows // PARTS
    part_res = n_loc // PARTS
    lanes = 128
    n_hi = rows // lanes
    n_lo = hid // n_hi

    me = lax.axis_index("dap")
    core = lax.rem(me, CORES)
    chip = me // CORES
    x, y = lax.rem(chip, side), chip // side
    pos_a = x * (1 - core) + y * core
    pos_b = y * (1 - core) + x * core

    def device(a, b, which):
        a, b = lax.rem(a, side), lax.rem(b, side)
        return ((b * (1 - core) + a * core) * side + a * (1 - core) + b * core) * CORES + which

    peers = {
        "A+": device(pos_a + 1, pos_b, core),
        "A-": device(pos_a + side - 1, pos_b, core),
        "B+": device(pos_a, pos_b + 1, core),
        "B-": device(pos_a, pos_b + side - 1, core),
        "D": device(pos_a, pos_b, 1 - core),
    }
    lane_of = {d: k for k, d in enumerate(peers)}
    slot = {unit: k for k, unit in enumerate(units)}
    part_index = {}
    for events in before:
        for event in events:
            part_index[event] = len(part_index)
    other_index = {name: k for k, name in enumerate(u[1] for u in units if u[0] == "other")}

    barrier = pltpu.get_barrier_semaphore()
    for peer in peers.values():
        pl.semaphore_signal(barrier, inc=1, device_id={"dap": peer}, device_id_type=MESH)

    m_copies = []
    for g in range(PARTS):
        span = pl.ds(g * part_res, part_res)
        m_copies.append(pltpu.make_async_copy(m_hbm.at[span], m_ref.at[span], m_sem.at[g]))
    small = [pltpu.make_async_copy(s, d, in_sem.at[k]) for k, (s, d) in enumerate((
        (scale_hbm, scale_ref), (offset_hbm, offset_ref), (wa_hbm, wa_ref), (ba_hbm, ba_ref), (wb_hbm, wb_ref),
        (bb_hbm, bb_ref), (bo_hbm, bo_ref)))]
    wo_copies = [pltpu.make_async_copy(wo_hbm.at[:, k], wo_ref.at[k], wo_sem.at[k]) for k in range(n_lo)]
    z_copy = pltpu.make_async_copy(z_hbm, z_ref, z_sem)
    for copy in m_copies[:1] + small + m_copies[1:] + wo_copies + [z_copy]:
        copy.start()

    sent = {d: 0 for d in peers}

    def send(direction, name_here, part, name_there):
        kind_there = "other" if direction == "D" else "own"
        src = slot["own", name_here] * rows + part * part_rows
        dst = slot[kind_there, name_there] * rows + part * part_rows
        sem = block_sem.at[other_index[name_there]] if direction == "D" else part_sem.at[part_index[name_there, part]]
        pltpu.make_async_remote_copy(
            src_ref=held.at[pl.ds(src, part_rows)],
            dst_ref=held.at[pl.ds(dst, part_rows)],
            send_sem=send_sem.at[lane_of[direction]],
            recv_sem=sem,
            device_id={"dap": peers[direction]},
            device_id_type=MESH,
        ).start()

    def pass_on(name, part):
        for direction, there in forwards(name, part, side):
            sent[direction] += 1
            send(direction, name, part, there)
        sent["D"] += 1
        send("D", name, part, name)

    def landed(ref, sem):
        pltpu.make_async_copy(ref, ref, sem).wait()

    def receive(name, part):
        start = slot["own", name] * rows + part * part_rows
        landed(held.at[pl.ds(start, part_rows)], part_sem.at[part_index[name, part]])
        pass_on(name, part)

    def receive_other(name):
        landed(held.at[pl.ds(slot["other", name] * rows, rows)], block_sem.at[other_index[name]])

    for copy in small:
        copy.wait()
    scale = column(scale_ref[...].astype(F32), msa_dim)
    offset = column(offset_ref[...].astype(F32), msa_dim)
    bias = jnp.concatenate([column(ba_ref[...].astype(F32), hid), column(bb_ref[...].astype(F32), hid)], axis=0)
    w_ab = jnp.concatenate([wa_ref[...], wb_ref[...]], axis=0)
    for g in range(PARTS):
        m_copies[g].wait()
        for r in range(g * part_res, (g + 1) * part_res):
            value = m_ref[r].astype(F32)
            mean = jnp.sum(value, axis=0, keepdims=True) * (1.0 / msa_dim)
            centred = value - mean
            var = jnp.sum(centred * centred, axis=0, keepdims=True) * (1.0 / msa_dim)
            normed = centred * lax.rsqrt(var + LN_EPS)
            normed = (normed * scale + offset).astype(BF16)
            both = jnp.dot(w_ab, normed, preferred_element_type=F32) + bias
            for c in range(0, hid, 8):
                for t in range(n_seq // lanes):
                    a_rows[t, pl.ds(c * n_loc + r, 8, stride=n_loc), :] = both[c:c + 8, t * lanes:(t + 1) * lanes]
            held[r * hid:(r + 1) * hid, :] = both[hid:].astype(BF16)
        if g == 0:
            pl.semaphore_wait(barrier, len(peers))
        else:
            pass_on((0, 0), g - 1)
    for t in range(n_seq // lanes):
        a_cols[t * lanes:(t + 1) * lanes, :] = a_rows[t].astype(BF16).T
    pass_on((0, 0), PARTS - 1)

    for copy in wo_copies:
        copy.wait()
    z_copy.wait()

    def out_start(kind, name):
        if kind == "own":
            owner = device(pos_a + name[0], pos_b + name[1], core)
        else:
            owner = device(pos_a + name[1], pos_b + name[0], 1 - core)
        return owner * n_loc

    starts = [out_start(*unit) for unit in units]
    actions = []
    for unit, events in zip(units, before):
        todo = [functools.partial(receive, *event) for event in events]
        if unit[0] == "other":
            todo.append(functools.partial(receive_other, unit[1]))
        actions.append(todo)

    inv_seq = 1.0 / n_seq
    bias_out = bo_ref[...].astype(F32)

    def step(index, carry):
        dispatch(index, 0, len(units), actions)
        start = starts[0]
        for k in range(1, len(units)):
            start = jnp.where(index == k, starts[k], start)
        here = pl.ds(pl.multiple_of(index * rows, rows), rows)
        for c in range(0, rows, 2 * lanes):
            prod = jnp.dot(held[here, :], a_cols[:, c:c + 2 * lanes], preferred_element_type=F32)
            outer[:, c:c + 2 * lanes] = (prod * inv_seq).astype(BF16)
        for j in range(n_loc):
            tile = jnp.concatenate([outer[j * hid:(j + 1) * hid, t * lanes:(t + 1) * lanes] for t in range(n_hi)], axis=0)
            turned = tile.T
            for k in range(n_lo):
                lhs[j * n_loc:(j + 1) * n_loc, k * lanes:(k + 1) * lanes] = turned[k * n_loc:(k + 1) * n_loc]
        w_all = wo_ref[...].reshape(n_lo * n_hi * hid, wo_ref.shape[-1])
        update = jnp.dot(lhs[...], w_all, preferred_element_type=F32) + bias_out
        for j in range(n_loc):
            for i in range(0, n_loc, 8):
                upd[pl.ds(i * n_loc + j, 8, stride=n_loc), :] = update[j * n_loc + i:j * n_loc + i + 8]
        cols = pl.ds(pl.multiple_of(start, n_loc), n_loc)
        total = z_ref[:, cols, :].astype(F32) + upd[...].reshape(n_loc, n_loc, upd.shape[-1])
        out_ref[:, cols, :] = total.astype(BF16)
        return carry

    lax.fori_loop(0, len(units), step, 0)

    for direction in peers:
        landed(held.at[pl.ds(0, sent[direction] * part_rows)], send_sem.at[lane_of[direction]])


def solution(mesh):
    row_spec = P(('batch', 'dap'))
    col_spec = P(None, ('batch', 'dap'))
    rep_spec = P()
    side = math.isqrt(mesh.shape['dap'] // CORES)
    units, before = plan(side)

    def local_update(z_rows, msa, ln_scale, ln_offset, w_a, b_a, w_b, b_b, w_out, b_out):
        n_seq, n_loc, msa_dim = msa.shape
        hid = w_a.shape[1]
        rows = n_loc * hid
        pair_dim = z_rows.shape[2]
        n_hi = rows // 128
        n_lo = hid // n_hi
        n_events = sum(len(events) for events in before)
        n_other = sum(unit[0] == "other" for unit in units)
        row = lambda v: v.reshape(1, -1)
        any_spec = pl.BlockSpec(memory_space=pl.ANY)
        vmem_spec = pl.BlockSpec(memory_space=pltpu.VMEM)
        call = pl.pallas_call(
            functools.partial(kernel, side, units, before),
            out_shape=jax.ShapeDtypeStruct(z_rows.shape, z_rows.dtype),
            in_specs=[any_spec] * 10,
            out_specs=vmem_spec,
            scratch_shapes=[
                pltpu.VMEM((n_loc, msa_dim, n_seq), BF16),
                pltpu.VMEM((1, msa_dim), BF16),
                pltpu.VMEM((1, msa_dim), BF16),
                pltpu.VMEM((hid, msa_dim), BF16),
                pltpu.VMEM((1, hid), BF16),
                pltpu.VMEM((hid, msa_dim), BF16),
                pltpu.VMEM((1, hid), BF16),
                pltpu.VMEM((n_lo, n_hi, hid, pair_dim), BF16),
                pltpu.VMEM((1, pair_dim), BF16),
                pltpu.VMEM(z_rows.shape, BF16),
                pltpu.VMEM((len(units) * rows, n_seq), BF16),
                pltpu.VMEM((n_seq // 128, rows, 128), F32),
                pltpu.VMEM((n_seq, rows), BF16),
                pltpu.VMEM((rows, rows), BF16),
                pltpu.VMEM((n_loc * n_loc, hid * hid), BF16),
                pltpu.VMEM((n_loc * n_loc, pair_dim), F32),
                pltpu.SemaphoreType.DMA((7,)),
                pltpu.SemaphoreType.DMA((PARTS,)),
                pltpu.SemaphoreType.DMA((n_lo,)),
                pltpu.SemaphoreType.DMA,
                pltpu.SemaphoreType.DMA((5,)),
                pltpu.SemaphoreType.DMA((n_events,)),
                pltpu.SemaphoreType.DMA((n_other,)),
            ],
            compiler_params=pltpu.CompilerParams(
                collective_id=0, has_side_effects=True, vmem_limit_bytes=56 * 1024 * 1024),
            name="outer_product_mean",
        )
        return call(z_rows, msa.transpose(1, 2, 0), row(ln_scale), row(ln_offset), w_a.T, row(b_a), w_b.T, row(b_b),
                    w_out.reshape(n_hi, n_lo, hid, pair_dim), row(b_out))

    return jax.shard_map(local_update, mesh=mesh, in_specs=(row_spec, col_spec) + (rep_spec,) * 8, out_specs=row_spec, check_vma=False)
```

time: 131 us -> 60.2 us (0.46)
  waiting for transfers between devices: 71.7 us -> 0 us
  Pallas kernels: 0 us -> 57 us
  matrix products: 42.7 us -> 0 us
  between operations: 13.6 us -> 0.01 us
  other arithmetic: 3.12 us -> 0 us
  local copies, waits for them, and re-layouts: 0.05 us -> 3.11 us
    all_gather x1 -> x0, waiting for transfers between devices: 71.6 us -> none  [local_update(): full_b = lax.all_gather(proj_b, 'dap', axis=1, tiled=True)]
    pallas_call x0 -> x1, Pallas kernels: none -> 57 us  [local_update(): call(z_rows, msa.transpose(1, 2, 0), row(ln_scale), row(ln_offset), w_a.T...]
    dot_general x3 -> x0, matrix products: 42.7 us -> none  [the longest x1 24.6 us: tile_body(): jnp.einsum('sic,sjd->icjd', a_tile, full_b, preferred_element_type=jnp.fl...]
    reduce_sum x2 -> x0, other arithmetic: 3.08 us -> none  [the longest x1 1.57 us: layer_norm(): var_val = jnp.mean(centred * centred, axis=-1, keepdims=True)]
    unnamed x20 -> x1, local copies, waits for them, and re-layouts: 0.05 us -> 3.11 us
  transfers between devices with their start and end apart: 1 -> 0, of which waited for: 1 -> 0; matrix products, arithmetic and copies ran while one was open for 0% -> 0% of each run, Pallas kernels for 0% -> 0%
where the time goes in v1:
time: 60.2 us; the launch traced here: 60.1 us
  Pallas kernels  57 us (95%)
  local copies, waits for them, and re-layouts  3.11 us (5%)
    pallas_call x1, Pallas kernels, local_update(): call(z_rows, msa.transpose(1, 2, 0), row(ln_scale), row(ln_offset), w_a.T...  57 us
    unnamed x1, local copies, waits for them, and re-layouts  3.11 us

profile of v1, /device:TPU:97, one launch (start us, length us, event | category | flops | bytes accessed | tf_op | source)
XLA Modules:
  0.0 60.1 jit_solution(17027145490227910344)
XLA Ops:
  0.0 57.0 %outer_product_mean.1 = bf16[16,512,128]{2,1,0:T(8,128)(2,1)} custom-call(bf16[16,512,128]{2,1,0:T(8,128)(2,1)} %z_hbm.1, bf16[16,64,512]{2,1,0:T(8,128)(2,1)} %bitcast.9, bf16[1,64]{1,0:T(2,128)(2,1)} %bitcast.13, bf16[1,64]{1,0:T(2,128)(2,1)} %bitcast.14, bf16[32,64]{1,0:T(8,128)(2,1)} %bitcast.11, bf16[1,32]{1,0:T(2,128)(2,1)} %bitcast.15, ...), custom_call_target="tpu_custom_call" | custom-call | tf_op jit(solution)/shard_map/outer_product_mean/pallas_call | solution.py:326
  57.0 3.1 %copy.12 = bf16[16,512,128]{2,1,0:T(8,128)(2,1)} copy(bf16[16,512,128]{2,1,0:T(8,128)(2,1)} %outer_product_mean.1) | data formatting | bytes 4194304

commit v2 on v1

--- a/solution.py
+++ b/solution.py
@@ -210,10 +210,10 @@
                 for t in range(n_seq // lanes):
                     a_rows[t, pl.ds(c * n_loc + r, 8, stride=n_loc), :] = both[c:c + 8, t * lanes:(t + 1) * lanes]
             held[r * hid:(r + 1) * hid, :] = both[hid:].astype(BF16)
-        if g == 0:
-            pl.semaphore_wait(barrier, len(peers))
-        else:
-            pass_on((0, 0), g - 1)
+            if r == part_res:
+                pl.semaphore_wait(barrier, len(peers))
+            if r and r % part_res == 0:
+                pass_on((0, 0), g - 1)
     for t in range(n_seq // lanes):
         a_cols[t * lanes:(t + 1) * lanes, :] = a_rows[t].astype(BF16).T
     pass_on((0, 0), PARTS - 1)
@@ -291,7 +291,7 @@
         vmem_spec = pl.BlockSpec(memory_space=pltpu.VMEM)
         call = pl.pallas_call(
             functools.partial(kernel, side, units, before),
-            out_shape=jax.ShapeDtypeStruct(z_rows.shape, z_rows.dtype),
+            out_shape=pltpu.VMEM(z_rows.shape, z_rows.dtype),
             in_specs=[any_spec] * 10,
             out_specs=vmem_spec,
             scratch_shapes=[

time: 60.2 us -> 56.7 us (0.942)
  local copies, waits for them, and re-layouts: 3.11 us -> 1.32 us
  Pallas kernels: 57 us -> 55.3 us
    unnamed x1, local copies, waits for them, and re-layouts: 3.11 us -> 1.32 us
    pallas_call x1, Pallas kernels: 57 us -> 55.3 us  [local_update(): call(z_rows, msa.transpose(1, 2, 0), row(ln_scale), row(ln_offset), w_a.T...]
where the time goes in v2:
time: 56.7 us; the launch traced here: 56.6 us
  Pallas kernels  55.3 us (98%)
  local copies, waits for them, and re-layouts  1.32 us (2%)
    pallas_call x1, Pallas kernels, local_update(): call(z_rows, msa.transpose(1, 2, 0), row(ln_scale), row(ln_offset), w_a.T...  55.3 us
    unnamed x1, local copies, waits for them, and re-layouts  1.32 us

profile of v2, /device:TPU:97, one launch (start us, length us, event | category | flops | bytes accessed | tf_op | source)
XLA Modules:
  0.0 56.6 jit_solution(8950236922350876603)
XLA Ops:
  0.0 55.3 %outer_product_mean.1 = bf16[16,512,128]{2,1,0:T(8,128)(2,1)S(1)} custom-call(bf16[16,512,128]{2,1,0:T(8,128)(2,1)} %z_hbm.1, bf16[16,64,512]{2,1,0:T(8,128)(2,1)} %bitcast.9, bf16[1,64]{1,0:T(2,128)(2,1)} %bitcast.13, bf16[1,64]{1,0:T(2,128)(2,1)} %bitcast.14, bf16[32,64]{1,0:T(8,128)(2,1)} %bitcast.11, bf16[1,32]{1,0:T(2,128)(2,1)} %bitcast.15, ...), custom_call_target="tpu_custom_call" | custom-call | tf_op jit(solution)/shard_map/outer_product_mean/pallas_call | solution.py:326
  55.3 1.3 %copy.12 = bf16[16,512,128]{2,1,0:T(8,128)(2,1)} copy(bf16[16,512,128]{2,1,0:T(8,128)(2,1)S(1)} %outer_product_mean.1) | data formatting | bytes 4194304

commit v3 on v2

--- a/solution.py
+++ b/solution.py
@@ -10,8 +10,8 @@
 
 LN_EPS = 1e-5
 CORES = 2
-PARTS = 4
-PARTNER_LAG = 3
+PARTS = 8
+PARTNER_LAG = 6
 MESH = pl.DeviceIdType.MESH
 F32 = jnp.float32
 BF16 = jnp.bfloat16

time: 56.7 us -> 57.2 us (level)
  no operation moved by 1% of the time
where the time goes in v3:
time: 57.2 us; the launch traced here: 57.1 us
  Pallas kernels  55.8 us (98%)
  local copies, waits for them, and re-layouts  1.32 us (2%)
    pallas_call x1, Pallas kernels, local_update(): call(z_rows, msa.transpose(1, 2, 0), row(ln_scale), row(ln_offset), w_a.T...  55.8 us
    unnamed x1, local copies, waits for them, and re-layouts  1.32 us

profile of v3, /device:TPU:97, one launch (start us, length us, event | category | flops | bytes accessed | tf_op | source)
XLA Modules:
  0.0 57.1 jit_solution(5534158096185003429)
XLA Ops:
  0.0 55.8 %outer_product_mean.1 = bf16[16,512,128]{2,1,0:T(8,128)(2,1)S(1)} custom-call(bf16[16,512,128]{2,1,0:T(8,128)(2,1)} %z_hbm.1, bf16[16,64,512]{2,1,0:T(8,128)(2,1)} %bitcast.9, bf16[1,64]{1,0:T(2,128)(2,1)} %bitcast.13, bf16[1,64]{1,0:T(2,128)(2,1)} %bitcast.14, bf16[32,64]{1,0:T(8,128)(2,1)} %bitcast.11, bf16[1,32]{1,0:T(2,128)(2,1)} %bitcast.15, ...), custom_call_target="tpu_custom_call" | custom-call | tf_op jit(solution)/shard_map/outer_product_mean/pallas_call | solution.py:326
  55.8 1.3 %copy.12 = bf16[16,512,128]{2,1,0:T(8,128)(2,1)} copy(bf16[16,512,128]{2,1,0:T(8,128)(2,1)S(1)} %outer_product_mean.1) | data formatting | bytes 4194304

commit v4 on v3

v4 whole, which is shorter than its diff:
```python
import functools
import heapq
import itertools
import math

import jax
import jax.numpy as jnp
from jax import lax
from jax.experimental import pallas as pl
from jax.experimental.pallas import tpu as pltpu
from jax.sharding import PartitionSpec as P

LN_EPS = 1e-5
CORES = 2
PART_SIZES = (2, 6, 8)
LINK_LATENCY = 5.0
PARTNER_LATENCY = 3.3
UNIT_TIME = 1.9
NORM_TIME = 0.26
MESH = pl.DeviceIdType.MESH
F32 = jnp.float32
BF16 = jnp.bfloat16
OWN = ("mine", 0, 0)


def forwards(name, part, over_link, side):
    kind, along, across = name
    low = sum(PART_SIZES[:part + 1]) * 2 <= sum(PART_SIZES)
    hops = []
    if not over_link and along == 0 and (kind == "other" or across == 0):
        hops.append(("+", (kind, side - 1, across)))
        hops.append(("-", (kind, 1, across)))
    elif over_link and along == side - 1 and low:
        hops.append(("+", (kind, along - 1, across)))
    elif over_link and along == 1 and not low:
        hops.append(("-", (kind, along + 1, across)))
    if over_link or name == OWN:
        hops.append(("core", ("other" if kind == "mine" else "mine", across, along)))
    return hops


def plan(side):
    tick = itertools.count()
    heap, free, events, ready = [], {"+": 0.0, "-": 0.0}, [], {}
    begin = NORM_TIME * sum(PART_SIZES) + UNIT_TIME
    ready[OWN] = begin
    for part in range(len(PART_SIZES)):
        heapq.heappush(heap, (NORM_TIME * sum(PART_SIZES[:part + 1]), next(tick), OWN, part, None))
    while heap:
        time, _, name, part, over_link = heapq.heappop(heap)
        if over_link is not None:
            ready[name] = max(ready.get(name, 0.0), time)
            if over_link or name[0] == "other":
                events.append((time, name, part, over_link))
        for direction, there in forwards(name, part, over_link, side):
            if direction == "core":
                at = time + PARTNER_LATENCY + 0.05 * PART_SIZES[part]
            else:
                free[direction] = max(free[direction], time) + PART_SIZES[part]
                at = free[direction] + LINK_LATENCY
            heapq.heappush(heap, (at, next(tick), there, part, direction != "core"))
    todo = sorted((time, name) for name, time in ready.items())
    units, before, waiting, now = [], [], [], begin
    while todo:
        if events and events[0][0] <= now:
            waiting.append(events.pop(0)[1:])
        elif todo[0][0] <= now:
            units.append(todo.pop(0)[1])
            before.append(waiting)
            waiting = []
            now += UNIT_TIME
        else:
            now = min([todo[0][0]] + [event[0] for event in events[:1]])
    return units, before


def column(row, size):
    shape = (size, size)
    eye = lax.broadcasted_iota(jnp.int32, shape, 0) == lax.broadcasted_iota(jnp.int32, shape, 1)
    return jnp.sum(jnp.where(eye, jnp.broadcast_to(row, shape), 0.0), axis=1, keepdims=True)


def dispatch(index, low, high, actions):
    if not any(actions[low:high]):
        return
    if high - low == 1:
        for action in actions[low]:
            action()
        return
    mid = (low + high) // 2
    if any(actions[low:mid]):
        pl.when(index < mid)(lambda: dispatch(index, low, mid, actions))
    if any(actions[mid:high]):
        pl.when(index >= mid)(lambda: dispatch(index, mid, high, actions))


def kernel(side, units, before, z_hbm, m_hbm, scale_hbm, offset_hbm, wa_hbm, ba_hbm, wb_hbm, bb_hbm, wo_hbm, bo_hbm, out_ref,
           m_ref, scale_ref, offset_ref, wa_ref, ba_ref, wb_ref, bb_ref, wo_ref, bo_ref, z_ref,
           held, a_rows, a_cols, outer, lhs, upd, in_sem, m_sem, wo_sem, z_sem, send_sem, part_sem, block_sem):
    n_loc, msa_dim, n_seq = m_ref.shape
    hid = wa_ref.shape[0]
    rows = n_loc * hid
    ends = list(itertools.accumulate(PART_SIZES))
    begins = [0] + ends[:-1]
    lanes = 128
    n_hi = rows // lanes
    n_lo = hid // n_hi

    me = lax.axis_index("dap")
    core = lax.rem(me, CORES)
    chip = me // CORES
    x, y = lax.rem(chip, side), chip // side
    pos_a = x * (1 - core) + y * core
    pos_b = y * (1 - core) + x * core

    def device(along, across, which):
        a, b = lax.rem(pos_a + along, side), lax.rem(pos_b + across, side)
        return ((b * (1 - core) + a * core) * side + a * (1 - core) + b * core) * CORES + which

    peers = {"+": device(1, 0, core), "-": device(side - 1, 0, core), "core": device(0, 0, 1 - core)}
    lane_of = {d: k for k, d in enumerate(peers)}
    slot = {name: k for k, name in enumerate(units)}
    part_index = {}
    for events in before:
        for name, part, _ in events:
            part_index[name, part] = len(part_index)
    whole = [name for name in units if name != OWN and (name, 0) not in part_index]
    block_index = {name: k for k, name in enumerate(whole)}

    barrier = pltpu.get_barrier_semaphore()
    for peer in peers.values():
        pl.semaphore_signal(barrier, inc=1, device_id={"dap": peer}, device_id_type=MESH)

    m_copies = []
    for k, (lo, hi) in enumerate(zip(begins, ends)):
        m_copies.append(pltpu.make_async_copy(m_hbm.at[lo:hi], m_ref.at[lo:hi], m_sem.at[k]))
    small = [pltpu.make_async_copy(s, d, in_sem.at[k]) for k, (s, d) in enumerate((
        (scale_hbm, scale_ref), (offset_hbm, offset_ref), (wa_hbm, wa_ref), (ba_hbm, ba_ref), (wb_hbm, wb_ref),
        (bb_hbm, bb_ref), (bo_hbm, bo_ref)))]
    wo_copies = [pltpu.make_async_copy(wo_hbm.at[:, k], wo_ref.at[k], wo_sem.at[k]) for k in range(n_lo)]
    z_copy = pltpu.make_async_copy(z_hbm, z_ref, z_sem)
    for copy in m_copies[:1] + small + m_copies[1:] + wo_copies + [z_copy]:
        copy.start()

    sent = {d: 0 for d in peers}

    def span(name, part):
        return pl.ds(slot[name] * rows + begins[part] * hid, PART_SIZES[part] * hid)

    def pass_on(name, part, over_link):
        for direction, there in forwards(name, part, over_link, side):
            sent[direction] += PART_SIZES[part] * hid
            pltpu.make_async_remote_copy(
                src_ref=held.at[span(name, part)],
                dst_ref=held.at[span(there, part)],
                send_sem=send_sem.at[lane_of[direction]],
                recv_sem=block_sem.at[block_index[there]] if there in block_index else part_sem.at[part_index[there, part]],
                device_id={"dap": peers[direction]},
                device_id_type=MESH,
            ).start()

    def landed(ref, sem):
        pltpu.make_async_copy(ref, ref, sem).wait()

    def receive(name, part, over_link):
        landed(held.at[span(name, part)], part_sem.at[part_index[name, part]])
        pass_on(name, part, over_link)

    def receive_block(name):
        landed(held.at[pl.ds(slot[name] * rows, rows)], block_sem.at[block_index[name]])

    for copy in small:
        copy.wait()
    scale = column(scale_ref[...].astype(F32), msa_dim)
    offset = column(offset_ref[...].astype(F32), msa_dim)
    bias = jnp.concatenate([column(ba_ref[...].astype(F32), hid), column(bb_ref[...].astype(F32), hid)], axis=0)
    w_ab = jnp.concatenate([wa_ref[...], wb_ref[...]], axis=0)
    for r in range(n_loc):
        if r in begins:
            m_copies[begins.index(r)].wait()
        value = m_ref[r].astype(F32)
        mean = jnp.sum(value, axis=0, keepdims=True) * (1.0 / msa_dim)
        centred = value - mean
        var = jnp.sum(centred * centred, axis=0, keepdims=True) * (1.0 / msa_dim)
        normed = centred * lax.rsqrt(var + LN_EPS)
        normed = (normed * scale + offset).astype(BF16)
        both = jnp.dot(w_ab, normed, preferred_element_type=F32) + bias
        for c in range(0, hid, 8):
            for t in range(n_seq // lanes):
                a_rows[t, pl.ds(c * n_loc + r, 8, stride=n_loc), :] = both[c:c + 8, t * lanes:(t + 1) * lanes]
        held[r * hid:(r + 1) * hid, :] = both[hid:].astype(BF16)
        if r in ends:
            if r == ends[0]:
                pl.semaphore_wait(barrier, len(peers))
            pass_on(OWN, ends.index(r), None)
    for t in range(n_seq // lanes):
        a_cols[t * lanes:(t + 1) * lanes, :] = a_rows[t].astype(BF16).T
    pass_on(OWN, len(ends) - 1, None)

    for copy in wo_copies:
        copy.wait()
    z_copy.wait()

    starts = [device(along, across, core if kind == "mine" else 1 - core) * n_loc for kind, along, across in units]
    actions = []
    for name, events in zip(units, before):
        todo = [functools.partial(receive, *event) for event in events]
        if name in block_index:
            todo.append(functools.partial(receive_block, name))
        actions.append(todo)

    inv_seq = 1.0 / n_seq
    bias_out = bo_ref[...].astype(F32)

    def step(index, carry):
        dispatch(index, 0, len(units), actions)
        start = starts[0]
        for k in range(1, len(units)):
            start = jnp.where(index == k, starts[k], start)
        here = pl.ds(pl.multiple_of(index * rows, rows), rows)
        for c in range(0, rows, 2 * lanes):
            prod = jnp.dot(held[here, :], a_cols[:, c:c + 2 * lanes], preferred_element_type=F32)
            outer[:, c:c + 2 * lanes] = (prod * inv_seq).astype(BF16)
        for j in range(n_loc):
            tile = jnp.concatenate([outer[j * hid:(j + 1) * hid, t * lanes:(t + 1) * lanes] for t in range(n_hi)], axis=0)
            turned = tile.T
            for k in range(n_lo):
                lhs[j * n_loc:(j + 1) * n_loc, k * lanes:(k + 1) * lanes] = turned[k * n_loc:(k + 1) * n_loc]
        w_all = wo_ref[...].reshape(n_lo * n_hi * hid, wo_ref.shape[-1])
        update = jnp.dot(lhs[...], w_all, preferred_element_type=F32) + bias_out
        for j in range(n_loc):
            for i in range(0, n_loc, 8):
                upd[pl.ds(i * n_loc + j, 8, stride=n_loc), :] = update[j * n_loc + i:j * n_loc + i + 8]
        cols = pl.ds(pl.multiple_of(start, n_loc), n_loc)
        total = z_ref[:, cols, :].astype(F32) + upd[...].reshape(n_loc, n_loc, upd.shape[-1])
        out_ref[:, cols, :] = total.astype(BF16)
        return carry

    lax.fori_loop(0, len(units), step, 0)

    for direction in peers:
        landed(held.at[pl.ds(0, sent[direction])], send_sem.at[lane_of[direction]])


def solution(mesh):
    row_spec = P(('batch', 'dap'))
    col_spec = P(None, ('batch', 'dap'))
    rep_spec = P()
    side = math.isqrt(mesh.shape['dap'] // CORES)
    units, before = plan(side)

    def local_update(z_rows, msa, ln_scale, ln_offset, w_a, b_a, w_b, b_b, w_out, b_out):
        n_seq, n_loc, msa_dim = msa.shape
        hid = w_a.shape[1]
        rows = n_loc * hid
        pair_dim = z_rows.shape[2]
        n_hi = rows // 128
        n_lo = hid // n_hi
        n_events = sum(len(events) for events in before)
        n_blocks = len(units) - 1 - n_events // len(PART_SIZES)
        row = lambda v: v.reshape(1, -1)
        any_spec = pl.BlockSpec(memory_space=pl.ANY)
        vmem_spec = pl.BlockSpec(memory_space=pltpu.VMEM)
        call = pl.pallas_call(
            functools.partial(kernel, side, units, before),
            out_shape=pltpu.VMEM(z_rows.shape, z_rows.dtype),
            in_specs=[any_spec] * 10,
            out_specs=vmem_spec,
            scratch_shapes=[
                pltpu.VMEM((n_loc, msa_dim, n_seq), BF16),
                pltpu.VMEM((1, msa_dim), BF16),
                pltpu.VMEM((1, msa_dim), BF16),
                pltpu.VMEM((hid, msa_dim), BF16),
                pltpu.VMEM((1, hid), BF16),
                pltpu.VMEM((hid, msa_dim), BF16),
                pltpu.VMEM((1, hid), BF16),
                pltpu.VMEM((n_lo, n_hi, hid, pair_dim), BF16),
                pltpu.VMEM((1, pair_dim), BF16),
                pltpu.VMEM(z_rows.shape, BF16),
                pltpu.VMEM((len(units) * rows, n_seq), BF16),
                pltpu.VMEM((n_seq // 128, rows, 128), F32),
                pltpu.VMEM((n_seq, rows), BF16),
                pltpu.VMEM((rows, rows), BF16),
                pltpu.VMEM((n_loc * n_loc, hid * hid), BF16),
                pltpu.VMEM((n_loc * n_loc, pair_dim), F32),
                pltpu.SemaphoreType.DMA((7,)),
                pltpu.SemaphoreType.DMA((len(PART_SIZES),)),
                pltpu.SemaphoreType.DMA((n_lo,)),
                pltpu.SemaphoreType.DMA,
                pltpu.SemaphoreType.DMA((3,)),
                pltpu.SemaphoreType.DMA((n_events,)),
                pltpu.SemaphoreType.DMA((n_blocks,)),
            ],
            compiler_params=pltpu.CompilerParams(
                collective_id=0, has_side_effects=True, vmem_limit_bytes=56 * 1024 * 1024),
            name="outer_product_mean",
        )
        return call(z_rows, msa.transpose(1, 2, 0), row(ln_scale), row(ln_offset), w_a.T, row(b_a), w_b.T, row(b_b),
                    w_out.reshape(n_hi, n_lo, hid, pair_dim), row(b_out))

    return jax.shard_map(local_update, mesh=mesh, in_specs=(row_spec, col_spec) + (rep_spec,) * 8, out_specs=row_spec, check_vma=False)
```

time: 57.2 us -> 55.5 us (0.970)
  Pallas kernels: 55.8 us -> 54.1 us
    pallas_call x1, Pallas kernels: 55.8 us -> 54.1 us  [local_update(): call(z_rows, msa.transpose(1, 2, 0), row(ln_scale), row(ln_offset), w_a.T...]
where the time goes in v4:
time: 55.5 us; the launch traced here: 55.4 us
  Pallas kernels  54.1 us (97%)
  local copies, waits for them, and re-layouts  1.32 us (2%)
    pallas_call x1, Pallas kernels, local_update(): call(z_rows, msa.transpose(1, 2, 0), row(ln_scale), row(ln_offset), w_a.T...  54.1 us
    unnamed x1, local copies, waits for them, and re-layouts  1.32 us

profile of v4, /device:TPU:97, one launch (start us, length us, event | category | flops | bytes accessed | tf_op | source)
XLA Modules:
  0.0 55.4 jit_solution(4643218165587121653)
XLA Ops:
  0.0 54.1 %outer_product_mean.1 = bf16[16,512,128]{2,1,0:T(8,128)(2,1)S(1)} custom-call(bf16[16,512,128]{2,1,0:T(8,128)(2,1)} %z_hbm.1, bf16[16,64,512]{2,1,0:T(8,128)(2,1)} %bitcast.9, bf16[1,64]{1,0:T(2,128)(2,1)} %bitcast.13, bf16[1,64]{1,0:T(2,128)(2,1)} %bitcast.14, bf16[32,64]{1,0:T(8,128)(2,1)} %bitcast.11, bf16[1,32]{1,0:T(2,128)(2,1)} %bitcast.15, ...), custom_call_target="tpu_custom_call" | custom-call | tf_op jit(solution)/shard_map/outer_product_mean/pallas_call | solution.py:298
  54.1 1.3 %copy.12 = bf16[16,512,128]{2,1,0:T(8,128)(2,1)} copy(bf16[16,512,128]{2,1,0:T(8,128)(2,1)S(1)} %outer_product_mean.1) | data formatting | bytes 4194304

commit v5 on v4

--- a/solution.py
+++ b/solution.py
@@ -12,10 +12,11 @@
 
 LN_EPS = 1e-5
 CORES = 2
-PART_SIZES = (2, 6, 8)
+HALVES = 2
+FIRST_PIECE = 2
 LINK_LATENCY = 5.0
-PARTNER_LATENCY = 3.3
-UNIT_TIME = 1.9
+PARTNER_LATENCY = 3.7
+UNIT_TIME = 1.0
 NORM_TIME = 0.26
 MESH = pl.DeviceIdType.MESH
 F32 = jnp.float32
@@ -23,42 +24,41 @@
 OWN = ("mine", 0, 0)
 
 
-def forwards(name, part, over_link, side):
+def forwards(name, half, over_link, side):
     kind, along, across = name
-    low = sum(PART_SIZES[:part + 1]) * 2 <= sum(PART_SIZES)
     hops = []
     if not over_link and along == 0 and (kind == "other" or across == 0):
         hops.append(("+", (kind, side - 1, across)))
         hops.append(("-", (kind, 1, across)))
-    elif over_link and along == side - 1 and low:
+    elif over_link and along == side - 1 and half == 0:
         hops.append(("+", (kind, along - 1, across)))
-    elif over_link and along == 1 and not low:
+    elif over_link and along == 1 and half == 1:
         hops.append(("-", (kind, along + 1, across)))
     if over_link or name == OWN:
         hops.append(("core", ("other" if kind == "mine" else "mine", across, along)))
     return hops
 
 
-def plan(side):
+def plan(side, n_loc):
     tick = itertools.count()
+    size = n_loc // HALVES
     heap, free, events, ready = [], {"+": 0.0, "-": 0.0}, [], {}
-    begin = NORM_TIME * sum(PART_SIZES) + UNIT_TIME
-    ready[OWN] = begin
-    for part in range(len(PART_SIZES)):
-        heapq.heappush(heap, (NORM_TIME * sum(PART_SIZES[:part + 1]), next(tick), OWN, part, None))
+    begin = NORM_TIME * n_loc + 1.5
+    for half in range(HALVES):
+        heapq.heappush(heap, (NORM_TIME * (half * size + FIRST_PIECE), next(tick), OWN, half, None))
+        ready[OWN, half] = begin
     while heap:
-        time, _, name, part, over_link = heapq.heappop(heap)
+        time, _, name, half, over_link = heapq.heappop(heap)
         if over_link is not None:
-            ready[name] = max(ready.get(name, 0.0), time)
-            if over_link or name[0] == "other":
-                events.append((time, name, part, over_link))
-        for direction, there in forwards(name, part, over_link, side):
+            ready[name, half] = time
+            events.append((time, name, half, over_link))
+        for direction, there in forwards(name, half, over_link, side):
             if direction == "core":
-                at = time + PARTNER_LATENCY + 0.05 * PART_SIZES[part]
+                at = time + PARTNER_LATENCY
             else:
-                free[direction] = max(free[direction], time) + PART_SIZES[part]
+                free[direction] = max(free[direction], time) + size
                 at = free[direction] + LINK_LATENCY
-            heapq.heappush(heap, (at, next(tick), there, part, direction != "core"))
+            heapq.heappush(heap, (at, next(tick), there, half, direction != "core"))
     todo = sorted((time, name) for name, time in ready.items())
     units, before, waiting, now = [], [], [], begin
     while todo:
@@ -96,12 +96,14 @@
 
 def kernel(side, units, before, z_hbm, m_hbm, scale_hbm, offset_hbm, wa_hbm, ba_hbm, wb_hbm, bb_hbm, wo_hbm, bo_hbm, out_ref,
            m_ref, scale_ref, offset_ref, wa_ref, ba_ref, wb_ref, bb_ref, wo_ref, bo_ref, z_ref,
-           held, a_rows, a_cols, outer, lhs, upd, in_sem, m_sem, wo_sem, z_sem, send_sem, part_sem, block_sem):
+           held, a_rows, a_cols, outer, lhs, upd, in_sem, m_sem, wo_sem, z_sem, send_sem, recv_sem):
     n_loc, msa_dim, n_seq = m_ref.shape
     hid = wa_ref.shape[0]
     rows = n_loc * hid
-    ends = list(itertools.accumulate(PART_SIZES))
-    begins = [0] + ends[:-1]
+    size = n_loc // HALVES
+    part_rows = size * hid
+    begins = [0, FIRST_PIECE] + [half * size for half in range(1, HALVES)]
+    ends = begins[1:] + [n_loc]
     lanes = 128
     n_hi = rows // lanes
     n_lo = hid // n_hi
@@ -120,13 +122,6 @@
     peers = {"+": device(1, 0, core), "-": device(side - 1, 0, core), "core": device(0, 0, 1 - core)}
     lane_of = {d: k for k, d in enumerate(peers)}
     slot = {name: k for k, name in enumerate(units)}
-    part_index = {}
-    for events in before:
-        for name, part, _ in events:
-            part_index[name, part] = len(part_index)
-    whole = [name for name in units if name != OWN and (name, 0) not in part_index]
-    block_index = {name: k for k, name in enumerate(whole)}
-
     barrier = pltpu.get_barrier_semaphore()
     for peer in peers.values():
         pl.semaphore_signal(barrier, inc=1, device_id={"dap": peer}, device_id_type=MESH)
@@ -144,17 +139,14 @@
 
     sent = {d: 0 for d in peers}
 
-    def span(name, part):
-        return pl.ds(slot[name] * rows + begins[part] * hid, PART_SIZES[part] * hid)
-
-    def pass_on(name, part, over_link):
-        for direction, there in forwards(name, part, over_link, side):
-            sent[direction] += PART_SIZES[part] * hid
+    def pass_on(name, half, over_link, lo=0, hi=size):
+        for direction, there in forwards(name, half, over_link, side):
+            sent[direction] += (hi - lo) * hid
             pltpu.make_async_remote_copy(
-                src_ref=held.at[span(name, part)],
-                dst_ref=held.at[span(there, part)],
+                src_ref=held.at[pl.ds(slot[name, half] * part_rows + lo * hid, (hi - lo) * hid)],
+                dst_ref=held.at[pl.ds(slot[there, half] * part_rows + lo * hid, (hi - lo) * hid)],
                 send_sem=send_sem.at[lane_of[direction]],
-                recv_sem=block_sem.at[block_index[there]] if there in block_index else part_sem.at[part_index[there, part]],
+                recv_sem=recv_sem.at[slot[there, half]],
                 device_id={"dap": peers[direction]},
                 device_id_type=MESH,
             ).start()
@@ -162,12 +154,14 @@
     def landed(ref, sem):
         pltpu.make_async_copy(ref, ref, sem).wait()
 
-    def receive(name, part, over_link):
-        landed(held.at[span(name, part)], part_sem.at[part_index[name, part]])
-        pass_on(name, part, over_link)
-
-    def receive_block(name):
-        landed(held.at[pl.ds(slot[name] * rows, rows)], block_sem.at[block_index[name]])
+    def receive(name, half, over_link):
+        index = slot[name, half]
+        landed(held.at[pl.ds(index * part_rows, part_rows)], recv_sem.at[index])
+        pass_on(name, half, over_link)
+
+    def send_own(piece):
+        half = begins[piece] // size
+        pass_on(OWN, half, None, begins[piece] - half * size, ends[piece] - half * size)
 
     for copy in small:
         copy.wait()
@@ -188,26 +182,23 @@
         for c in range(0, hid, 8):
             for t in range(n_seq // lanes):
                 a_rows[t, pl.ds(c * n_loc + r, 8, stride=n_loc), :] = both[c:c + 8, t * lanes:(t + 1) * lanes]
-        held[r * hid:(r + 1) * hid, :] = both[hid:].astype(BF16)
+        row = slot[OWN, r // size] * part_rows + r % size * hid
+        held[row:row + hid, :] = both[hid:].astype(BF16)
         if r in ends:
             if r == ends[0]:
                 pl.semaphore_wait(barrier, len(peers))
-            pass_on(OWN, ends.index(r), None)
+            send_own(ends.index(r))
     for t in range(n_seq // lanes):
         a_cols[t * lanes:(t + 1) * lanes, :] = a_rows[t].astype(BF16).T
-    pass_on(OWN, len(ends) - 1, None)
+    send_own(len(ends) - 1)
 
     for copy in wo_copies:
         copy.wait()
     z_copy.wait()
 
-    starts = [device(along, across, core if kind == "mine" else 1 - core) * n_loc for kind, along, across in units]
-    actions = []
-    for name, events in zip(units, before):
-        todo = [functools.partial(receive, *event) for event in events]
-        if name in block_index:
-            todo.append(functools.partial(receive_block, name))
-        actions.append(todo)
+    starts = [device(along, across, core if kind == "mine" else 1 - core) * n_loc + half * size
+              for (kind, along, across), half in units]
+    actions = [[functools.partial(receive, *event) for event in events] for events in before]
 
     inv_seq = 1.0 / n_seq
     bias_out = bo_ref[...].astype(F32)
@@ -217,22 +208,22 @@
         start = starts[0]
         for k in range(1, len(units)):
             start = jnp.where(index == k, starts[k], start)
-        here = pl.ds(pl.multiple_of(index * rows, rows), rows)
+        here = pl.ds(pl.multiple_of(index * part_rows, part_rows), part_rows)
         for c in range(0, rows, 2 * lanes):
             prod = jnp.dot(held[here, :], a_cols[:, c:c + 2 * lanes], preferred_element_type=F32)
             outer[:, c:c + 2 * lanes] = (prod * inv_seq).astype(BF16)
-        for j in range(n_loc):
+        for j in range(size):
             tile = jnp.concatenate([outer[j * hid:(j + 1) * hid, t * lanes:(t + 1) * lanes] for t in range(n_hi)], axis=0)
             turned = tile.T
             for k in range(n_lo):
                 lhs[j * n_loc:(j + 1) * n_loc, k * lanes:(k + 1) * lanes] = turned[k * n_loc:(k + 1) * n_loc]
         w_all = wo_ref[...].reshape(n_lo * n_hi * hid, wo_ref.shape[-1])
         update = jnp.dot(lhs[...], w_all, preferred_element_type=F32) + bias_out
-        for j in range(n_loc):
+        for j in range(size):
             for i in range(0, n_loc, 8):
-                upd[pl.ds(i * n_loc + j, 8, stride=n_loc), :] = update[j * n_loc + i:j * n_loc + i + 8]
-        cols = pl.ds(pl.multiple_of(start, n_loc), n_loc)
-        total = z_ref[:, cols, :].astype(F32) + upd[...].reshape(n_loc, n_loc, upd.shape[-1])
+                upd[pl.ds(i * size + j, 8, stride=size), :] = update[j * n_loc + i:j * n_loc + i + 8]
+        cols = pl.ds(pl.multiple_of(start, size), size)
+        total = z_ref[:, cols, :].astype(F32) + upd[...].reshape(n_loc, size, upd.shape[-1])
         out_ref[:, cols, :] = total.astype(BF16)
         return carry
 
@@ -247,8 +238,6 @@
     col_spec = P(None, ('batch', 'dap'))
     rep_spec = P()
     side = math.isqrt(mesh.shape['dap'] // CORES)
-    units, before = plan(side)
-
     def local_update(z_rows, msa, ln_scale, ln_offset, w_a, b_a, w_b, b_b, w_out, b_out):
         n_seq, n_loc, msa_dim = msa.shape
         hid = w_a.shape[1]
@@ -256,8 +245,7 @@
         pair_dim = z_rows.shape[2]
         n_hi = rows // 128
         n_lo = hid // n_hi
-        n_events = sum(len(events) for events in before)
-        n_blocks = len(units) - 1 - n_events // len(PART_SIZES)
+        units, before = plan(side, n_loc)
         row = lambda v: v.reshape(1, -1)
         any_spec = pl.BlockSpec(memory_space=pl.ANY)
         vmem_spec = pl.BlockSpec(memory_space=pltpu.VMEM)
@@ -277,19 +265,18 @@
                 pltpu.VMEM((n_lo, n_hi, hid, pair_dim), BF16),
                 pltpu.VMEM((1, pair_dim), BF16),
                 pltpu.VMEM(z_rows.shape, BF16),
-                pltpu.VMEM((len(units) * rows, n_seq), BF16),
+                pltpu.VMEM((len(units) * rows // HALVES, n_seq), BF16),
                 pltpu.VMEM((n_seq // 128, rows, 128), F32),
                 pltpu.VMEM((n_seq, rows), BF16),
-                pltpu.VMEM((rows, rows), BF16),
-                pltpu.VMEM((n_loc * n_loc, hid * hid), BF16),
-                pltpu.VMEM((n_loc * n_loc, pair_dim), F32),
+                pltpu.VMEM((rows // HALVES, rows), BF16),
+                pltpu.VMEM((n_loc * n_loc // HALVES, hid * hid), BF16),
+                pltpu.VMEM((n_loc * n_loc // HALVES, pair_dim), F32),
                 pltpu.SemaphoreType.DMA((7,)),
-                pltpu.SemaphoreType.DMA((len(PART_SIZES),)),
+                pltpu.SemaphoreType.DMA((HALVES + 1,)),
                 pltpu.SemaphoreType.DMA((n_lo,)),
                 pltpu.SemaphoreType.DMA,
                 pltpu.SemaphoreType.DMA((3,)),
-                pltpu.SemaphoreType.DMA((n_events,)),
-                pltpu.SemaphoreType.DMA((n_blocks,)),
+                pltpu.SemaphoreType.DMA((len(units),)),
             ],
             compiler_params=pltpu.CompilerParams(
                 collective_id=0, has_side_effects=True, vmem_limit_bytes=56 * 1024 * 1024),

time: 55.5 us -> 56.5 us (1.018)
  Pallas kernels: 54.1 us -> 55.1 us
    pallas_call x1, Pallas kernels: 54.1 us -> 55.1 us  [local_update(): call(z_rows, msa.transpose(1, 2, 0), row(ln_scale), row(ln_offset), w_a.T...]
where the time goes in v5:
time: 56.5 us; the launch traced here: 56.4 us
  Pallas kernels  55.1 us (98%)
  local copies, waits for them, and re-layouts  1.32 us (2%)
    pallas_call x1, Pallas kernels, local_update(): call(z_rows, msa.transpose(1, 2, 0), row(ln_scale), row(ln_offset), w_a.T...  55.1 us
    unnamed x1, local copies, waits for them, and re-layouts  1.32 us

profile of v5, /device:TPU:97, one launch (start us, length us, event | category | flops | bytes accessed | tf_op | source)
XLA Modules:
  0.0 56.4 jit_solution(18026543014278022142)
XLA Ops:
  0.0 55.1 %outer_product_mean.1 = bf16[16,512,128]{2,1,0:T(8,128)(2,1)S(1)} custom-call(bf16[16,512,128]{2,1,0:T(8,128)(2,1)} %z_hbm.1, bf16[16,64,512]{2,1,0:T(8,128)(2,1)} %bitcast.9, bf16[1,64]{1,0:T(2,128)(2,1)} %bitcast.13, bf16[1,64]{1,0:T(2,128)(2,1)} %bitcast.14, bf16[32,64]{1,0:T(8,128)(2,1)} %bitcast.11, bf16[1,32]{1,0:T(2,128)(2,1)} %bitcast.15, ...), custom_call_target="tpu_custom_call" | custom-call | tf_op jit(solution)/shard_map/outer_product_mean/pallas_call | solution.py:285
  55.1 1.3 %copy.12 = bf16[16,512,128]{2,1,0:T(8,128)(2,1)} copy(bf16[16,512,128]{2,1,0:T(8,128)(2,1)S(1)} %outer_product_mean.1) | data formatting | bytes 4194304

commit v6 on v5

--- a/solution.py
+++ b/solution.py
@@ -15,8 +15,9 @@
 HALVES = 2
 FIRST_PIECE = 2
 LINK_LATENCY = 5.0
-PARTNER_LATENCY = 3.7
-UNIT_TIME = 1.0
+PARTNER_LATENCY = 5.0
+PARTNER_TIME = 0.3
+UNIT_TIME = 1.1
 NORM_TIME = 0.26
 MESH = pl.DeviceIdType.MESH
 F32 = jnp.float32
@@ -42,7 +43,7 @@
 def plan(side, n_loc):
     tick = itertools.count()
     size = n_loc // HALVES
-    heap, free, events, ready = [], {"+": 0.0, "-": 0.0}, [], {}
+    heap, free, events, ready = [], {"+": 0.0, "-": 0.0, "core": 0.0}, [], {}
     begin = NORM_TIME * n_loc + 1.5
     for half in range(HALVES):
         heapq.heappush(heap, (NORM_TIME * (half * size + FIRST_PIECE), next(tick), OWN, half, None))
@@ -53,11 +54,9 @@
             ready[name, half] = time
             events.append((time, name, half, over_link))
         for direction, there in forwards(name, half, over_link, side):
-            if direction == "core":
-                at = time + PARTNER_LATENCY
-            else:
-                free[direction] = max(free[direction], time) + size
-                at = free[direction] + LINK_LATENCY
+            busy, latency = (PARTNER_TIME, PARTNER_LATENCY) if direction == "core" else (1.0, LINK_LATENCY)
+            free[direction] = max(free[direction], time) + busy * size
+            at = free[direction] + latency
             heapq.heappush(heap, (at, next(tick), there, half, direction != "core"))
     todo = sorted((time, name) for name, time in ready.items())
     units, before, waiting, now = [], [], [], begin

time: 56.5 us -> 55.3 us (0.979)
  Pallas kernels: 55.1 us -> 53.9 us
    pallas_call x1, Pallas kernels: 55.1 us -> 53.9 us  [local_update(): call(z_rows, msa.transpose(1, 2, 0), row(ln_scale), row(ln_offset), w_a.T...]
where the time goes in v6:
time: 55.3 us; the launch traced here: 55.2 us
  Pallas kernels  53.9 us (97%)
  local copies, waits for them, and re-layouts  1.32 us (2%)
    pallas_call x1, Pallas kernels, local_update(): call(z_rows, msa.transpose(1, 2, 0), row(ln_scale), row(ln_offset), w_a.T...  53.9 us
    unnamed x1, local copies, waits for them, and re-layouts  1.32 us

profile of v6, /device:TPU:97, one launch (start us, length us, event | category | flops | bytes accessed | tf_op | source)
XLA Modules:
  0.0 55.2 jit_solution(12574718189050614547)
XLA Ops:
  0.0 53.9 %outer_product_mean.1 = bf16[16,512,128]{2,1,0:T(8,128)(2,1)S(1)} custom-call(bf16[16,512,128]{2,1,0:T(8,128)(2,1)} %z_hbm.1, bf16[16,64,512]{2,1,0:T(8,128)(2,1)} %bitcast.9, bf16[1,64]{1,0:T(2,128)(2,1)} %bitcast.13, bf16[1,64]{1,0:T(2,128)(2,1)} %bitcast.14, bf16[32,64]{1,0:T(8,128)(2,1)} %bitcast.11, bf16[1,32]{1,0:T(2,128)(2,1)} %bitcast.15, ...), custom_call_target="tpu_custom_call" | custom-call | tf_op jit(solution)/shard_map/outer_product_mean/pallas_call | solution.py:284
  53.9 1.3 %copy.12 = bf16[16,512,128]{2,1,0:T(8,128)(2,1)} copy(bf16[16,512,128]{2,1,0:T(8,128)(2,1)S(1)} %outer_product_mean.1) | data formatting | bytes 4194304
